TPU v7x, 32 devices: a whole 2x2x4 slice. The times are simulated.
32 devices in a mesh: ta: 2 (over x), gx: 16 (over z, y, core).
Axes of the slice: x: 2, y: 2, z: 4, core: 2. Of those that a mesh axis runs over, the one named last changes fastest.
Arguments:
- voltages: bfloat16 [2, 128, 2, 256, 512], P('ta', 'gx'), may hold values from -6 to 6
- weights: bfloat16 [2, 256, 2, 512, 64], P(None, 'gx'), may hold values from -0.125 to 0.125
Outputs:
- spectra: float32 [256, 2, 512, 64], P(None, None, 'gx', 'ta')
All inputs are finite; a program needn't handle non-finite values.
Results may differ from a plain program's by a relative error of at most 0.0003.
Values may be sent and summed in bfloat16 or wider, within the bound.
A program may use at most 64 MiB of HBM per device.

v0:
```python
import jax
import jax.numpy as jnp
from jax import lax
from jax.sharding import PartitionSpec as P


def beam_power(voltage, weight_block):
    antennas = weight_block.shape[3]
    beam_count = weight_block.shape[2]
    powers = []
    for side_index in range(2):
        real_w = weight_block[side_index, 0]
        imag_w = weight_block[side_index, 1]
        upper_rows = jnp.stack([real_w, -imag_w], axis=-1).reshape(beam_count, 2 * antennas)
        bottom_half_rows = jnp.stack([imag_w, real_w], axis=-1).reshape(beam_count, 2 * antennas)
        matrix = jnp.concatenate([upper_rows, bottom_half_rows], 0)
        signal = voltage[side_index * antennas : (side_index + 1) * antennas].reshape(
            2 * antennas, -1
        )
        beam_voltage_field = jnp.dot(matrix, signal, preferred_element_type=jnp.float32)
        power = (
            beam_voltage_field[:beam_count] * beam_voltage_field[:beam_count]
            + beam_voltage_field[beam_count:] * beam_voltage_field[beam_count:]
        )
        powers.append(power.reshape(beam_count, -1, 8).sum(-1))
    return jnp.stack(powers, 0)


def channel_powers(turned, weights):

    def one_channel(column):
        voltage = lax.dynamic_index_in_dim(turned, column, 2, keepdims=False)
        weight_block = lax.dynamic_index_in_dim(weights, column, 1, keepdims=False)
        return beam_power(voltage, weight_block)

    return lax.map(one_channel, jnp.arange(turned.shape[2], dtype=jnp.int32))


def on_device(voltages, weights):
    turned = lax.all_to_all(voltages, "gx", split_axis=3, concat_axis=1, tiled=True)
    partial_power_value = channel_powers(turned[0], weights)
    relaid = lax.all_to_all(partial_power_value, "gx", split_axis=2, concat_axis=0, tiled=True)
    return lax.psum_scatter(relaid, "ta", scatter_dimension=3, tiled=True)


def solution(mesh):
    in_specs = (P("ta", "gx", None, None, None), P(None, "gx", None, None, None))
    out_specs = P(None, None, "gx", "ta")
    return jax.shard_map(
        on_device, mesh=mesh, in_specs=in_specs, out_specs=out_specs, check_vma=False
    )
```

profile of v0, /device:TPU:25, one launch (start us, length us, event | category | flops | bytes accessed | tf_op | source)
XLA Modules:
  0.0 488.2 jit_solution(4160567813515500975)
XLA Ops:
  6.5 6.5 %copy.34 = bf16[1,8,2,256,512]{4,1,2,0,3:T(8,128)(2,1)} copy(bf16[1,8,2,256,512]{4,3,2,1,0:T(8,128)(2,1)} %param.4) | data formatting | bytes 8388608 | tf_op args[0]
  13.0 6.4 %all-to-all-start = ((bf16[1,8,2,256,512]{4,1,2,0,3:T(8,128)(2,1)}), bf16[1,8,2,256,512]{4,1,2,0,3:T(8,128)(2,1)}, u32[]{:S(2)}, u32[]{:S(2)}) async-start(bf16[1,8,2,256,512]{4,1,2,0,3:T(8,128)(2,1)} %copy.34), calls=%async_computation | async-start | bytes 8388608 | tf_op jit(solution)/shard_map/all_to_all | solution.py:40
  19.4 86.4 %all-to-all-done = bf16[1,8,2,256,512]{4,1,2,0,3:T(8,128)(2,1)} async-done(((bf16[1,8,2,256,512]{4,1,2,0,3:T(8,128)(2,1)}), bf16[1,8,2,256,512]{4,1,2,0,3:T(8,128)(2,1)}, u32[]{:S(2)}, u32[]{:S(2)}) %all-to-all-start) | async-done | bytes 4194336 | tf_op jit(solution)/shard_map/all_to_all | solution.py:40
  105.8 8.5 %copy.35 = bf16[1,16,8,2,16,512]{5,3,2,1,4,0:T(2,128)(2,1)} copy(bf16[1,16,8,2,16,512]{5,2,3,4,1,0:T(8,128)(2,1)} %bitcast.12) | data formatting | bytes 8388608 | tf_op jit(solution)/shard_map/all_to_all | solution.py:40
  114.4 132.5 %while.10 = (s32[]{:T(128)}, f32[16,2,512,64]{2,3,1,0:T(8,128)}, s32[16]{0:T(128)S(1)}, bf16[2,16,2,512,64]{3,4,2,1,0:T(8,128)(2,1)}, bf16[128,2,16,512]{3,1,0,2...) while((s32[]{:T(128)}, f32[16,2,512,64]{2,3,1,0:T(8,128)}, s32[16]{0:T(128)S(1)}, ...), condition=%wide.region_3.4_spmd, body=%wide.region_0.3_spmd.sunk | while | flops 271908864 | bytes 15335599 | solution.py:36
  114.4 0.6 dynamic_slice.16
  116.8 1.2 constant_dynamic-slice_fusion.3
  118.1 1.0 dynamic-slice_bitcast_fusion.2
  121.9 0.7 fusion.40
  122.6 0.6 dynamic_slice.16
  125.1 1.2 constant_dynamic-slice_fusion.3
  126.4 1.0 dynamic-slice_bitcast_fusion.2
  130.2 0.7 fusion.40
  133.4 1.2 constant_dynamic-slice_fusion.3
  134.6 1.0 dynamic-slice_bitcast_fusion.2
  138.5 0.7 fusion.40
  141.7 1.2 constant_dynamic-slice_fusion.3
  142.9 1.0 dynamic-slice_bitcast_fusion.2
  146.8 0.7 fusion.40
  149.9 1.2 constant_dynamic-slice_fusion.3
  151.2 1.0 dynamic-slice_bitcast_fusion.2
  155.1 0.7 fusion.40
  158.2 1.2 constant_dynamic-slice_fusion.3
  159.5 1.0 dynamic-slice_bitcast_fusion.2
  163.3 0.7 fusion.40
  166.5 1.2 constant_dynamic-slice_fusion.3
  167.8 1.0 dynamic-slice_bitcast_fusion.2
  171.6 0.7 fusion.40
  174.8 1.2 constant_dynamic-slice_fusion.3
  176.1 1.0 dynamic-slice_bitcast_fusion.2
  179.9 0.7 fusion.40
  183.1 1.2 constant_dynamic-slice_fusion.3
  184.4 1.0 dynamic-slice_bitcast_fusion.2
  188.2 0.7 fusion.40
  191.4 1.2 constant_dynamic-slice_fusion.3
  192.7 1.0 dynamic-slice_bitcast_fusion.2
  196.5 0.7 fusion.40
  199.7 1.2 constant_dynamic-slice_fusion.3
  201.0 1.0 dynamic-slice_bitcast_fusion.2
  204.8 0.7 fusion.40
  208.0 1.2 constant_dynamic-slice_fusion.3
  209.2 1.0 dynamic-slice_bitcast_fusion.2
  213.1 0.7 fusion.40
  216.2 1.2 constant_dynamic-slice_fusion.3
  217.5 1.0 dynamic-slice_bitcast_fusion.2
  221.3 0.7 fusion.40
  224.5 1.2 constant_dynamic-slice_fusion.3
  225.8 1.0 dynamic-slice_bitcast_fusion.2
  229.6 0.7 fusion.40
  232.8 1.2 constant_dynamic-slice_fusion.3
  234.1 1.0 dynamic-slice_bitcast_fusion.2
  237.9 0.7 fusion.40
  241.0 1.2 constant_dynamic-slice_fusion.3
  242.3 1.0 dynamic-slice_bitcast_fusion.2
  246.1 0.7 fusion.40
  246.9 12.2 %copy.37 = f32[16,2,512,64]{3,1,0,2:T(2,128)} copy(f32[16,2,512,64]{2,3,1,0:T(8,128)} %get-tuple-element.32) | data formatting | bytes 8388608 | tf_op jit(solution)/shard_map/while | solution.py:36
  259.1 15.1 %reshape.49 = f32[16,1,65536]{2,1,0:T(1,128)} reshape(f32[512,16,2,64]{3,2,1,0:T(2,128)} %bitcast.77) | data formatting | bytes 8388608
  274.2 102.2 %all_to_all.33 = f32[16,1,65536]{2,1,0:T(1,128)} all-to-all(f32[16,1,65536]{2,1,0:T(1,128)} %reshape.49), channel_id=1, replica_groups=mesh['ta'=2,'gx'=16] {'gx'}, dimensions={0} | all-to-all | bytes 8388608 | tf_op jit(solution)/shard_map/all_to_all | solution.py:42
  377.0 13.7 %reduce = f32[16,65536]{1,0:T(8,128)} reduce(f32[16,1,65536]{2,1,0:T(1,128)} %all_to_all.33, f32[]{:T(128)} %broadcast), dimensions={1}, to_apply=%all_to_all.27.reduce_sub_computation | reduce | bytes 8388612 | tf_op jit(solution)/shard_map/all_to_all | solution.py:42
  390.7 9.7 %reshape.50 = f32[512,16,2,64]{3,2,1,0:T(2,128)} reshape(f32[16,65536]{1,0:T(8,128)} %reduce) | data formatting | bytes 8388608
  400.4 13.1 %copy.38 = f32[16,2,16,32,64]{4,3,1,0,2:T(8,128)} copy(f32[16,2,16,32,64]{4,1,0,3,2:T(2,128)} %bitcast.78) | data formatting | bytes 8388608 | tf_op jit(solution)/shard_map/all_to_all | solution.py:42
  413.4 8.7 %copy.39 = f32[256,2,32,64]{0,2,1,3:T(8,128)} copy(f32[256,2,32,64]{3,2,1,0:T(8,128)} %bitcast.79) | data formatting | bytes 8388608 | tf_op jit(solution)/shard_map/all_to_all | solution.py:42
  422.1 55.1 %reduce-scatter.2.cloned.1.call-done = f32[256,2,32,32]{0,2,1,3:T(8,128)} async-done(((f32[256,2,32,64]{0,2,1,3:T(8,128)}), f32[256,2,32,32]{0,2,1,3:T(8,128)}) %reduce-scatter.2.cloned.1.call-update) | async-done | bytes 2097168 | tf_op jit(solution)/shard_map/reduce_scatter | solution.py:43
  477.2 4.1 copy.40
  (291 shorter events, 54.5 us)
Async XLA Ops:
  13.0 92.8 %all-to-all-start = ((bf16[1,8,2,256,512]{4,1,2,0,3:T(8,128)(2,1)}), bf16[1,8,2,256,512]{4,1,2,0,3:T(8,128)(2,1)}, u32[]{:S(2)}, u32[]{:S(2)}) async-start(bf16[1,8,2,256,512]{4,1,2,0,3:T(8,128)(2,1)} %copy.34), calls=%async_computation | async-start | bytes 8388608 | tf_op jit(solution)/shard_map/all_to_all | solution.py:40
  19.3 457.9 %reduce-scatter.2.cloned.1.call-start = ((), (), s32[]{:S(2)}) async-start(), calls=%async_computation.3 | async-start | bytes 6291456 | tf_op jit(solution)/shard_map/reduce_scatter | solution.py:43
Sparse Core Ops, SparseCore 0:
  422.2 54.9 reduce-scatter.1
where the time goes:
time: 492 us; the launch traced here: 488 us
  waiting for transfers between devices  142 us (29%)
  local copies, waits for them, and re-layouts  137 us (28%)
  blocking collectives  102 us (21%)
  other arithmetic  41.3 us (8%)
  loops' own time  31.5 us (6%)
  matrix products  15.2 us (3%)
  between operations  13.4 us (3%)
  starting transfers between devices  6.39 us (1%)
    all_to_all x1, blocking collectives, on_device(): lax.all_to_all(partial_power_value, 'gx', split_axis=2, concat_axis=0, ti...  102 us
    all_to_all x1, waiting for transfers between devices, on_device(): lax.all_to_all(voltages, 'gx', split_axis=3, concat_axis=1, tiled=True)  86.4 us
    reduce_scatter x1, waiting for transfers between devices, on_device(): return lax.psum_scatter(relaid, 'ta', scatter_dimension=3, tiled=True)  55.1 us
    another operation x1, loops' own time, channel_powers(): return lax.map(one_channel, jnp.arange(turned.shape[2], dtype=jnp.int32))  31.5 us
    unnamed x3, local copies, waits for them, and re-layouts  31.2 us
    all_to_all x3, local copies, waits for them, and re-layouts, on_device(): lax.all_to_all(partial_power_value, 'gx', split_axis=2, concat_axis=0, ti...  22.2 us
    slice x16, local copies, waits for them, and re-layouts, beam_power(): voltage[side_index * antennas:(side_index + 1) * antennas]  18.5 us
    squeeze x16, local copies, waits for them, and re-layouts, one_channel(): weight_block = lax.dynamic_index_in_dim(weights, column, 1, keepdims=False)  15.6 us
  transfers between devices with their start and end apart: 2, of which 2 were waited for; matrix products, arithmetic and copies ran while one was open for 0% of the time, Pallas kernels for 0%

commit v1 on v0

--- a/solution.py
+++ b/solution.py
@@ -1,7 +1,14 @@
+import functools
+
 import jax
 import jax.numpy as jnp
 from jax import lax
+from jax.experimental import pallas as pl
+from jax.experimental.pallas import tpu as pltpu
 from jax.sharding import PartitionSpec as P
+
+MESH = pl.DeviceIdType.MESH
+CHUNKS = 4
 
 
 def beam_power(voltage, weight_block):
@@ -36,16 +43,224 @@
     return lax.map(one_channel, jnp.arange(turned.shape[2], dtype=jnp.int32))
 
 
-def on_device(voltages, weights):
+def plain_on_device(voltages, weights):
     turned = lax.all_to_all(voltages, "gx", split_axis=3, concat_axis=1, tiled=True)
     partial_power_value = channel_powers(turned[0], weights)
     relaid = lax.all_to_all(partial_power_value, "gx", split_axis=2, concat_axis=0, tiled=True)
     return lax.psum_scatter(relaid, "ta", scatter_dimension=3, tiled=True)
 
 
+def kernel(
+    nx, ng, v_ref, w_hbm, turn_ref, mix_ref, gather_ref, out_ref,
+    sbuf, vrecv, w_ref, pbuf, w_sem, vsend, vget, psend, pget,
+):
+    x = lax.axis_index("ta")
+    g = lax.axis_index("gx")
+    me = x * ng + g
+    n = nx * ng
+    rows = v_ref.shape[0] * v_ref.shape[1]
+    chans = v_ref.shape[2] // ng
+    half = v_ref.shape[3] // nx
+    per = chans // CHUNKS
+    group = ng // 2
+    antennas2 = group * rows
+    beams = w_ref.shape[3]
+
+    w_copy = pltpu.make_async_copy(w_hbm, w_ref, w_sem)
+    w_copy.start()
+
+    barrier = pltpu.get_barrier_semaphore()
+
+    def greet(i, _):
+        d = lax.rem(me + i, n)
+        pl.semaphore_signal(
+            barrier, inc=1, device_id=(d // ng, lax.rem(d, ng)), device_id_type=MESH
+        )
+        return 0
+
+    lax.fori_loop(1, n, greet, 0)
+
+    def turn(b, _):
+        start = pl.multiple_of(b * chans, chans)
+        block = v_ref[:, :, pl.ds(start, chans), :].reshape(rows * chans, nx * half)
+        turned = jnp.dot(turn_ref[...], block, preferred_element_type=jnp.float32)
+        turned = turned.astype(jnp.bfloat16).reshape(CHUNKS, per, rows, nx * half)
+        for k in range(nx):
+            sbuf[:, k * ng + b] = turned[:, :, :, k * half : (k + 1) * half]
+        return 0
+
+    lax.fori_loop(0, ng, turn, 0)
+    pl.semaphore_wait(barrier, n - 1)
+
+    for k in range(CHUNKS):
+        pltpu.make_async_copy(sbuf.at[k, me], vrecv.at[k, me], vget.at[k]).start()
+
+        def send(i, _, k=k):
+            d = lax.rem(me + i, n)
+            pltpu.make_async_remote_copy(
+                src_ref=sbuf.at[k, d],
+                dst_ref=vrecv.at[k, me],
+                send_sem=vsend.at[k],
+                recv_sem=vget.at[k],
+                device_id=(d // ng, lax.rem(d, ng)),
+                device_id_type=MESH,
+            ).start()
+            return 0
+
+        lax.fori_loop(1, n, send, 0)
+
+    w_copy.wait()
+
+    def chunk_step(k, _):
+        pltpu.make_async_copy(vrecv.at[k], vrecv.at[k], vget.at[k]).wait()
+
+        def channel(step, _):
+            c = step // 2
+            q = lax.rem(step, 2)
+            col = k * per + c
+            w = jnp.concatenate([w_ref[q, col, 0], w_ref[q, col, 1]], axis=1)
+            power = None
+            for h in range(nx):
+                first = h * ng + q * group
+                v = vrecv[k, pl.ds(first, group), c].reshape(antennas2, half)
+                mixed = jnp.dot(mix_ref[...], v, preferred_element_type=jnp.float32)
+                mixed = mixed.astype(jnp.bfloat16)
+                re = jnp.dot(w, mixed[:antennas2], preferred_element_type=jnp.float32)
+                im = jnp.dot(w, mixed[antennas2:], preferred_element_type=jnp.float32)
+                part = re * re + im * im
+                power = part if power is None else power + part
+            own = beams // ng
+            packs = own // 8
+            power = power.reshape(ng, packs, 8, half)
+            total = None
+            for m in range(packs):
+                p = power[:, m].reshape(ng * 8, half)
+                high = p.astype(jnp.bfloat16)
+                low = (p - high.astype(jnp.float32)).astype(jnp.bfloat16)
+                t = jnp.dot(high, gather_ref[m], preferred_element_type=jnp.float32)
+                t += jnp.dot(low, gather_ref[m], preferred_element_type=jnp.float32)
+                total = t if total is None else total + t
+            pbuf[k, :, q, c] = total.reshape(ng, 8, 128)
+            return 0
+
+        lax.fori_loop(0, 2 * per, channel, 0)
+
+        pltpu.make_async_copy(pbuf.at[k, g], out_ref.at[g, k], pget).start()
+
+        def send(i, _):
+            d = lax.rem(g + i, ng)
+            pltpu.make_async_remote_copy(
+                src_ref=pbuf.at[k, d],
+                dst_ref=out_ref.at[g, k],
+                send_sem=psend,
+                recv_sem=pget,
+                device_id=(x, d),
+                device_id_type=MESH,
+            ).start()
+            return 0
+
+        lax.fori_loop(1, ng, send, 0)
+        return 0
+
+    lax.fori_loop(0, CHUNKS, chunk_step, 0)
+
+    pltpu.make_async_copy(out_ref, out_ref, pget).wait()
+    for k in range(CHUNKS):
+        sent = sbuf.at[k, pl.ds(0, n - 1)]
+        pltpu.make_async_copy(sent, sent, vsend.at[k]).wait()
+    sent = pbuf.at[:, pl.ds(0, ng - 1)]
+    pltpu.make_async_copy(sent, sent, psend).wait()
+
+
+def spread_kernel(in_ref, out_ref):
+    chunks, per = in_ref.shape[1], in_ref.shape[3]
+    bins = out_ref.shape[3]
+    for m in range(128 // bins):
+        for k in range(chunks):
+            for q in range(2):
+                out_ref[k * per : (k + 1) * per, q, m * 8 : (m + 1) * 8, :] = in_ref[
+                    0, k, q, :, :, m * bins : (m + 1) * bins
+                ]
+
+
+def on_device(nx, ng, voltages, weights):
+    v = voltages[0]
+    streams, parts, channels, samples = v.shape
+    rows, chans, half = streams * parts, channels // ng, samples // nx
+    per = chans // CHUNKS
+    group = ng // 2
+    antennas = group * streams
+    beams = weights.shape[3]
+    own = beams // ng
+    packs = own // 8
+    bins = half // 8
+
+    i = jnp.arange(rows * chans)[:, None]
+    j = jnp.arange(rows * chans)[None, :]
+    turn = ((j % chans == i // rows) & (j // chans == i % rows)).astype(jnp.bfloat16)
+    i = jnp.arange(4 * antennas)[:, None]
+    j = jnp.arange(2 * antennas)[None, :]
+    block = i // antennas
+    wants = 2 * (i % antennas) + jnp.where((block == 0) | (block == 3), 0, 1)
+    mix = jnp.where(j == wants, jnp.where(block == 1, -1.0, 1.0), 0.0).astype(jnp.bfloat16)
+    m = jnp.arange(packs)[:, None, None]
+    s = jnp.arange(half)[None, :, None]
+    lane = jnp.arange(128)[None, None, :]
+    gather = (lane == m * bins + s // 8).astype(jnp.bfloat16)
+
+    vmem = pl.BlockSpec(memory_space=pltpu.VMEM)
+    anywhere = pl.BlockSpec(memory_space=pl.ANY)
+    packed = pl.pallas_call(
+        functools.partial(kernel, nx, ng),
+        out_shape=jax.ShapeDtypeStruct((ng, CHUNKS, 2, per, 8, 128), jnp.float32),
+        in_specs=[vmem, anywhere, vmem, vmem, vmem],
+        out_specs=anywhere,
+        scratch_shapes=[
+            pltpu.VMEM((CHUNKS, nx * ng, per, rows, half), jnp.bfloat16),
+            pltpu.VMEM((CHUNKS, nx * ng, per, rows, half), jnp.bfloat16),
+            pltpu.VMEM(weights.shape, jnp.bfloat16),
+            pltpu.VMEM((CHUNKS, ng, 2, per, 8, 128), jnp.float32),
+            pltpu.SemaphoreType.DMA,
+            pltpu.SemaphoreType.DMA((CHUNKS,)),
+            pltpu.SemaphoreType.DMA((CHUNKS,)),
+            pltpu.SemaphoreType.DMA,
+            pltpu.SemaphoreType.DMA,
+        ],
+        compiler_params=pltpu.CompilerParams(
+            collective_id=0, has_side_effects=True, vmem_limit_bytes=56 * 1024 * 1024
+        ),
+    )(v, weights, turn, mix, gather)
+
+    return pl.pallas_call(
+        spread_kernel,
+        grid=(ng,),
+        out_shape=jax.ShapeDtypeStruct((channels, 2, own, bins), jnp.float32),
+        in_specs=[pl.BlockSpec((1, CHUNKS, 2, per, 8, 128), lambda b: (b, 0, 0, 0, 0, 0))],
+        out_specs=pl.BlockSpec((chans, 2, own, bins), lambda b: (b, 0, 0, 0)),
+    )(packed)
+
+
 def solution(mesh):
+    nx, ng = mesh.shape["ta"], mesh.shape["gx"]
+
+    def body(voltages, weights):
+        _, streams, parts, channels, samples = voltages.shape
+        rows, chans, half = streams * parts, channels // ng, samples // nx
+        own = weights.shape[3] // ng
+        fits = (
+            nx == 2
+            and rows % 16 == 0
+            and chans % 16 == 0
+            and half % 128 == 0
+            and own % 8 == 0
+            and (own // 8) * (half // 8) == 128
+        )
+        if fits:
+            return on_device(nx, ng, voltages, weights)
+        return plain_on_device(voltages, weights)
+
     in_specs = (P("ta", "gx", None, None, None), P(None, "gx", None, None, None))
     out_specs = P(None, None, "gx", "ta")
     return jax.shard_map(
-        on_device, mesh=mesh, in_specs=in_specs, out_specs=out_specs, check_vma=False
+        body, mesh=mesh, in_specs=in_specs, out_specs=out_specs, check_vma=False
     )

time: 492 us -> 175 us (0.36)
  Pallas kernels: 0 us -> 155 us
  waiting for transfers between devices: 142 us -> 0 us
  local copies, waits for them, and re-layouts: 137 us -> 15.7 us
  blocking collectives: 102 us -> 0 us
  other arithmetic: 41.3 us -> 2.55 us
  loops' own time: 31.5 us -> 0 us
  matrix products: 15.2 us -> 0 us
  between operations: 13.4 us -> 0.03 us
  starting transfers between devices: 6.39 us -> 0 us
    pallas_call x0 -> x2, Pallas kernels: none -> 155 us  [the longest x1 143 us: on_device(): pl.pallas_call(functools.partial(kernel, nx, ng), out_shape=jax.ShapeDtyp...]
    all_to_all x1 -> x0, blocking collectives: 102 us -> none  [on_device(): lax.all_to_all(partial_power_value, 'gx', split_axis=2, concat_axis=0, ti...]
    all_to_all x1 -> x0, waiting for transfers between devices: 86.4 us -> none  [on_device(): lax.all_to_all(voltages, 'gx', split_axis=3, concat_axis=1, tiled=True)]
    reduce_scatter x1 -> x0, waiting for transfers between devices: 55.1 us -> none  [on_device(): return lax.psum_scatter(relaid, 'ta', scatter_dimension=3, tiled=True)]
    another operation x1 -> x0, loops' own time: 31.5 us -> none  [channel_powers(): return lax.map(one_channel, jnp.arange(turned.shape[2], dtype=jnp.int32))]
    all_to_all x4 -> x0, local copies, waits for them, and re-layouts: 30.8 us -> none  [the longest x3 22.2 us: on_device(): lax.all_to_all(partial_power_value, 'gx', split_axis=2, concat_axis=0, ti...]
    unnamed x3 -> x1, local copies, waits for them, and re-layouts: 31.2 us -> 8.38 us
    slice x16 -> x0, local copies, waits for them, and re-layouts: 18.5 us -> none  [beam_power(): voltage[side_index * antennas:(side_index + 1) * antennas]]
  transfers between devices with their start and end apart: 2 -> 0, of which waited for: 2 -> 0; matrix products, arithmetic and copies ran while one was open for 0% -> 0% of each run, Pallas kernels for 0% -> 0%
where the time goes in v1:
time: 175 us; the launch traced here: 173 us
  Pallas kernels  155 us (89%)
  local copies, waits for them, and re-layouts  15.7 us (9%)
  other arithmetic  2.55 us (1%)
    pallas_call x1, Pallas kernels, on_device(): pl.pallas_call(functools.partial(kernel, nx, ng), out_shape=jax.ShapeDtyp...  143 us
    pallas_call x1, Pallas kernels, on_device(): pl.pallas_call(spread_kernel, grid=(ng,), out_shape=jax.ShapeDtypeStruct(...  11.5 us
    unnamed x1, local copies, waits for them, and re-layouts  8.38 us
    pallas_call x1, local copies, waits for them, and re-layouts, on_device(): pl.pallas_call(spread_kernel, grid=(ng,), out_shape=jax.ShapeDtypeStruct(...  7.37 us

profile of v1, /device:TPU:25, one launch (start us, length us, event | category | flops | bytes accessed | tf_op | source)
XLA Modules:
  0.0 172.9 jit_solution(5168754987650918066)
XLA Ops:
  0.0 0.1 broadcast_add_fusion
  0.1 0.8 select_convert_fusion.mix_ref
  0.9 0.8 and_convert_fusion.turn_ref
  1.7 0.9 fusion.gather_ref
  2.6 8.4 %copy.3.w_hbm = bf16[2,16,2,512,64]{4,3,2,1,0:T(8,128)(2,1)} copy(bf16[2,16,2,512,64]{3,4,2,1,0:T(8,128)(2,1)} %param.3) | data formatting | bytes 8388608 | tf_op args[1]
  11.0 143.0 %shard_map.28.in_ref = f32[16,4,2,4,8,128]{5,4,3,2,1,0:T(8,128)} custom-call(bf16[8,2,256,512]{3,2,1,0:T(8,128)(2,1)} %bitcast.1, bf16[2,16,2,512,64]{4,3,2,1,0:T(8,128)(2,1)} %copy.3.w_hbm, bf16[256,256]{1,0:T(8,128)(2,1)} %and_convert_fusion.turn_ref, bf16[256,128]{1,0:T(8,128)(2,1)} %select_convert_fusion.mix_ref, bf16[4,256,128]{2,1,0:T(8,128)(2,1)} %fusion.gather_ref), custom_call_target="tpu_custom_call" | custom-call | tf_op jit(solution)/shard_map/pallas_call | solution.py:213
  154.0 11.5 %shard_map.29 = f32[256,2,32,32]{3,2,1,0:T(8,128)} custom-call(f32[16,4,2,4,8,128]{5,4,3,2,1,0:T(8,128)} %shard_map.28.in_ref), custom_call_target="tpu_custom_call" | custom-call | tf_op jit(solution)/shard_map/pallas_call | solution.py:234
  165.5 7.4 %copy.4 = f32[256,2,32,32]{0,3,2,1:T(8,128)} copy(f32[256,2,32,32]{3,2,1,0:T(8,128)} %shard_map.29) | data formatting | bytes 4194304 | tf_op jit(solution)/shard_map/pallas_call | solution.py:234
  (5 shorter events, 0.0 us)

commit v2 on v1

--- a/solution.py
+++ b/solution.py
@@ -2,11 +2,13 @@
 
 import jax
 import jax.numpy as jnp
+import numpy as np
 from jax import lax
 from jax.experimental import pallas as pl
 from jax.experimental.pallas import tpu as pltpu
 from jax.sharding import PartitionSpec as P
 
+BF16 = np.dtype(jnp.bfloat16)
 MESH = pl.DeviceIdType.MESH
 CHUNKS = 4
 
@@ -64,7 +66,7 @@
     per = chans // CHUNKS
     group = ng // 2
     antennas2 = group * rows
-    beams = w_ref.shape[3]
+    beams = w_ref.shape[4]
 
     w_copy = pltpu.make_async_copy(w_hbm, w_ref, w_sem)
     w_copy.start()
@@ -118,7 +120,7 @@
             c = step // 2
             q = lax.rem(step, 2)
             col = k * per + c
-            w = jnp.concatenate([w_ref[q, col, 0], w_ref[q, col, 1]], axis=1)
+            w = w_ref[q, col].reshape(antennas2, beams).T
             power = None
             for h in range(nx):
                 first = h * ng + q * group
@@ -145,13 +147,13 @@
 
         lax.fori_loop(0, 2 * per, channel, 0)
 
-        pltpu.make_async_copy(pbuf.at[k, g], out_ref.at[g, k], pget).start()
+        pltpu.make_async_copy(pbuf.at[k, g], out_ref.at[:, g, k], pget).start()
 
         def send(i, _):
             d = lax.rem(g + i, ng)
             pltpu.make_async_remote_copy(
                 src_ref=pbuf.at[k, d],
-                dst_ref=out_ref.at[g, k],
+                dst_ref=out_ref.at[:, g, k],
                 send_sem=psend,
                 recv_sem=pget,
                 device_id=(x, d),
@@ -173,14 +175,11 @@
 
 
 def spread_kernel(in_ref, out_ref):
-    chunks, per = in_ref.shape[1], in_ref.shape[3]
-    bins = out_ref.shape[3]
-    for m in range(128 // bins):
-        for k in range(chunks):
-            for q in range(2):
-                out_ref[k * per : (k + 1) * per, q, m * 8 : (m + 1) * 8, :] = in_ref[
-                    0, k, q, :, :, m * bins : (m + 1) * bins
-                ]
+    channels, bins = out_ref.shape[3], out_ref.shape[2]
+    for r in range(8):
+        lanes = in_ref[0, pl.ds(r, channels, stride=8), :].T
+        for m in range(128 // bins):
+            out_ref[0, m * 8 + r] = lanes[m * bins : (m + 1) * bins]
 
 
 def on_device(nx, ng, voltages, weights):
@@ -195,30 +194,31 @@
     packs = own // 8
     bins = half // 8
 
-    i = jnp.arange(rows * chans)[:, None]
-    j = jnp.arange(rows * chans)[None, :]
-    turn = ((j % chans == i // rows) & (j // chans == i % rows)).astype(jnp.bfloat16)
-    i = jnp.arange(4 * antennas)[:, None]
-    j = jnp.arange(2 * antennas)[None, :]
+    i = np.arange(rows * chans)[:, None]
+    j = np.arange(rows * chans)[None, :]
+    turn = ((j % chans == i // rows) & (j // chans == i % rows)).astype(BF16)
+    i = np.arange(4 * antennas)[:, None]
+    j = np.arange(2 * antennas)[None, :]
     block = i // antennas
-    wants = 2 * (i % antennas) + jnp.where((block == 0) | (block == 3), 0, 1)
-    mix = jnp.where(j == wants, jnp.where(block == 1, -1.0, 1.0), 0.0).astype(jnp.bfloat16)
-    m = jnp.arange(packs)[:, None, None]
-    s = jnp.arange(half)[None, :, None]
-    lane = jnp.arange(128)[None, None, :]
-    gather = (lane == m * bins + s // 8).astype(jnp.bfloat16)
-
+    wants = 2 * (i % antennas) + np.where((block == 0) | (block == 3), 0, 1)
+    mix = np.where(j == wants, np.where(block == 1, -1.0, 1.0), 0.0).astype(BF16)
+    m = np.arange(packs)[:, None, None]
+    s = np.arange(half)[None, :, None]
+    lane = np.arange(128)[None, None, :]
+    gather = (lane == m * bins + s // 8).astype(BF16)
+
+    turned_weights = jnp.swapaxes(weights, 3, 4)
     vmem = pl.BlockSpec(memory_space=pltpu.VMEM)
     anywhere = pl.BlockSpec(memory_space=pl.ANY)
     packed = pl.pallas_call(
         functools.partial(kernel, nx, ng),
-        out_shape=jax.ShapeDtypeStruct((ng, CHUNKS, 2, per, 8, 128), jnp.float32),
+        out_shape=jax.ShapeDtypeStruct((2, ng, CHUNKS, per, 8, 128), jnp.float32),
         in_specs=[vmem, anywhere, vmem, vmem, vmem],
         out_specs=anywhere,
         scratch_shapes=[
             pltpu.VMEM((CHUNKS, nx * ng, per, rows, half), jnp.bfloat16),
             pltpu.VMEM((CHUNKS, nx * ng, per, rows, half), jnp.bfloat16),
-            pltpu.VMEM(weights.shape, jnp.bfloat16),
+            pltpu.VMEM(turned_weights.shape, jnp.bfloat16),
             pltpu.VMEM((CHUNKS, ng, 2, per, 8, 128), jnp.float32),
             pltpu.SemaphoreType.DMA,
             pltpu.SemaphoreType.DMA((CHUNKS,)),
@@ -229,15 +229,16 @@
         compiler_params=pltpu.CompilerParams(
             collective_id=0, has_side_effects=True, vmem_limit_bytes=56 * 1024 * 1024
         ),
-    )(v, weights, turn, mix, gather)
-
-    return pl.pallas_call(
+    )(v, turned_weights, turn, mix, gather)
+
+    spread = pl.pallas_call(
         spread_kernel,
-        grid=(ng,),
-        out_shape=jax.ShapeDtypeStruct((channels, 2, own, bins), jnp.float32),
-        in_specs=[pl.BlockSpec((1, CHUNKS, 2, per, 8, 128), lambda b: (b, 0, 0, 0, 0, 0))],
-        out_specs=pl.BlockSpec((chans, 2, own, bins), lambda b: (b, 0, 0, 0)),
-    )(packed)
+        grid=(2,),
+        out_shape=jax.ShapeDtypeStruct((2, own, bins, channels), jnp.float32),
+        in_specs=[pl.BlockSpec((1, channels * 8, 128), lambda q: (q, 0, 0))],
+        out_specs=pl.BlockSpec((1, own, bins, channels), lambda q: (q, 0, 0, 0)),
+    )(packed.reshape(2, channels * 8, 128))
+    return spread.transpose(3, 0, 1, 2)
 
 
 def solution(mesh):

time: 175 us -> 147 us (0.84)
  local copies, waits for them, and re-layouts: 15.7 us -> 0 us
  Pallas kernels: 155 us -> 146 us
  other arithmetic: 2.55 us -> 0 us
    pallas_call x1, Pallas kernels: 11.5 us -> 2.9 us  [on_device(): pl.pallas_call(spread_kernel, grid=(2,), out_shape=jax.ShapeDtypeStruct((...]
    unnamed x1 -> x0, local copies, waits for them, and re-layouts: 8.38 us -> none
    pallas_call x1 -> x0, local copies, waits for them, and re-layouts: 7.37 us -> none  [on_device(): pl.pallas_call(spread_kernel, grid=(ng,), out_shape=jax.ShapeDtypeStruct(...]
    convert_element_type x3 -> x0, other arithmetic: 2.46 us -> none  [the longest x1 0.9 us: on_device(): gather = (lane == m * bins + s // 8).astype(jnp.bfloat16)]
where the time goes in v2:
time: 147 us; the launch traced here: 146 us
  Pallas kernels  146 us (99%)
    pallas_call x1, Pallas kernels, on_device(): pl.pallas_call(functools.partial(kernel, nx, ng), out_shape=jax.ShapeDtyp...  143 us

profile of v2, /device:TPU:25, one launch (start us, length us, event | category | flops | bytes accessed | tf_op | source)
XLA Modules:
  0.0 145.9 jit_solution(3383857075981357012)
XLA Ops:
  0.0 143.0 %shard_map.55 = f32[2,16,4,4,8,128]{5,4,3,2,1,0:T(8,128)} custom-call(bf16[8,2,256,512]{3,2,1,0:T(8,128)(2,1)} %bitcast.5, bf16[2,16,2,64,512]{4,3,2,1,0:T(8,128)(2,1)} %bitcast.6, bf16[256,256]{1,0:T(8,128)(2,1)} %constant.6.clone.turn_ref, bf16[256,128]{1,0:T(8,128)(2,1)} %constant.7.clone.mix_ref, bf16[4,256,128]{2,1,0:T(8,128)(2,1)} %constant.8.clone.gather_ref), custom_call_target="tpu_custom_call" | custom-call | tf_op jit(solution)/shard_map/pallas_call | solution.py:213
  143.0 2.9 %shard_map.56 = f32[2,32,32,256]{3,2,1,0:T(8,128)} custom-call(f32[2,2048,128]{2,1,0:T(8,128)} %bitcast.4), custom_call_target="tpu_custom_call" | custom-call | tf_op jit(solution)/shard_map/pallas_call | solution.py:234

commit v3 on v2

--- a/solution.py
+++ b/solution.py
@@ -11,6 +11,8 @@
 BF16 = np.dtype(jnp.bfloat16)
 MESH = pl.DeviceIdType.MESH
 CHUNKS = 4
+PIECES = 4
+LEAD = 2
 
 
 def beam_power(voltage, weight_block):
@@ -54,7 +56,8 @@
 
 def kernel(
     nx, ng, v_ref, w_hbm, turn_ref, mix_ref, gather_ref, out_ref,
-    sbuf, vrecv, w_ref, pbuf, w_sem, vsend, vget, psend, pget,
+    sbuf, vrecv, w_ref, pbuf,
+    w_sem, wsend, wz, relay_sem, wx, vsend, vget, psend, pget,
 ):
     x = lax.axis_index("ta")
     g = lax.axis_index("gx")
@@ -67,8 +70,15 @@
     group = ng // 2
     antennas2 = group * rows
     beams = w_ref.shape[4]
-
-    w_copy = pltpu.make_async_copy(w_hbm, w_ref, w_sem)
+    side = g // group
+    u = lax.rem(g, group)
+    partner = lax.rem(g + group, ng)
+    steps = 2 * CHUNKS
+    dests = nx * group
+    mine = x * group + u
+    piece = chans // nx // PIECES
+
+    w_copy = pltpu.make_async_copy(w_hbm.at[side], w_ref.at[0], w_sem)
     w_copy.start()
 
     barrier = pltpu.get_barrier_semaphore()
@@ -82,49 +92,98 @@
 
     lax.fori_loop(1, n, greet, 0)
 
-    def turn(b, _):
-        start = pl.multiple_of(b * chans, chans)
-        block = v_ref[:, :, pl.ds(start, chans), :].reshape(rows * chans, nx * half)
-        turned = jnp.dot(turn_ref[...], block, preferred_element_type=jnp.float32)
-        turned = turned.astype(jnp.bfloat16).reshape(CHUNKS, per, rows, nx * half)
-        for k in range(nx):
-            sbuf[:, k * ng + b] = turned[:, :, :, k * half : (k + 1) * half]
-        return 0
-
-    lax.fori_loop(0, ng, turn, 0)
-    pl.semaphore_wait(barrier, n - 1)
-
-    for k in range(CHUNKS):
-        pltpu.make_async_copy(sbuf.at[k, me], vrecv.at[k, me], vget.at[k]).start()
-
-        def send(i, _, k=k):
-            d = lax.rem(me + i, n)
+    def turn_side(which):
+        base = lax.rem(which + side, 2) * CHUNKS
+
+        def turn(i, _):
+            start = pl.multiple_of((which * group + i) * chans, chans)
+            block = v_ref[:, :, pl.ds(start, chans), :].reshape(rows * chans, nx * half)
+            turned = jnp.dot(turn_ref[...], block, preferred_element_type=jnp.float32)
+            turned = turned.astype(jnp.bfloat16).reshape(CHUNKS, per, rows, nx * half)
+            for k in range(nx):
+                sbuf[pl.ds(base, CHUNKS), k * group + i] = turned[
+                    :, :, :, k * half : (k + 1) * half
+                ]
+            return 0
+
+        lax.fori_loop(0, group, turn, 0)
+
+    def send_voltages(k):
+        pltpu.make_async_copy(sbuf.at[k, mine], vrecv.at[k, mine], vget.at[k]).start()
+
+        def send(i, _):
+            d = lax.rem(mine + i, dests)
             pltpu.make_async_remote_copy(
                 src_ref=sbuf.at[k, d],
-                dst_ref=vrecv.at[k, me],
+                dst_ref=vrecv.at[k, mine],
                 send_sem=vsend.at[k],
                 recv_sem=vget.at[k],
-                device_id=(d // ng, lax.rem(d, ng)),
+                device_id=(d // group, side * group + lax.rem(d, group)),
                 device_id_type=MESH,
             ).start()
             return 0
 
-        lax.fori_loop(1, n, send, 0)
-
+        lax.fori_loop(1, dests, send, 0)
+
+    def send_weights(i):
+        span = pl.ds((x * PIECES + i) * piece, piece)
+        pltpu.make_async_remote_copy(
+            src_ref=w_hbm.at[1 - side, span],
+            dst_ref=w_ref.at[1, span],
+            send_sem=wsend,
+            recv_sem=wz.at[i],
+            device_id=(x, partner),
+            device_id_type=MESH,
+        ).start()
+
+    def relay_weights(i):
+        block = w_ref.at[1, pl.ds((x * PIECES + i) * piece, piece)]
+        pltpu.make_async_copy(block, block, wz.at[i]).wait()
+        pltpu.make_async_remote_copy(
+            src_ref=block,
+            dst_ref=block,
+            send_sem=relay_sem,
+            recv_sem=wx,
+            device_id=(1 - x, g),
+            device_id_type=MESH,
+        ).start()
+
+    turn_side(side)
+    pl.semaphore_wait(barrier, n - 1)
+    for k in range(LEAD):
+        send_voltages(k)
+        send_weights(k)
+    turn_side(1 - side)
     w_copy.wait()
 
-    def chunk_step(k, _):
+    def step(k, _):
         pltpu.make_async_copy(vrecv.at[k], vrecv.at[k], vget.at[k]).wait()
 
-        def channel(step, _):
-            c = step // 2
-            q = lax.rem(step, 2)
-            col = k * per + c
-            w = w_ref[q, col].reshape(antennas2, beams).T
+        @pl.when(k + LEAD < steps)
+        def _():
+            send_voltages(k + LEAD)
+
+        @pl.when(k + LEAD < PIECES)
+        def _():
+            send_weights(k + LEAD)
+
+        @pl.when((k >= 1) & (k <= PIECES))
+        def _():
+            relay_weights(k - 1)
+
+        @pl.when(k == CHUNKS)
+        def _():
+            other = w_ref.at[1, pl.ds((1 - x) * PIECES * piece, PIECES * piece)]
+            pltpu.make_async_copy(other, other, wx).wait()
+
+        which = k // CHUNKS
+        part_of = lax.rem(k, CHUNKS)
+
+        def channel(c, _):
+            w = w_ref[which, part_of * per + c].reshape(antennas2, beams).T
             power = None
             for h in range(nx):
-                first = h * ng + q * group
-                v = vrecv[k, pl.ds(first, group), c].reshape(antennas2, half)
+                v = vrecv[k, h * group : (h + 1) * group, c].reshape(antennas2, half)
                 mixed = jnp.dot(mix_ref[...], v, preferred_element_type=jnp.float32)
                 mixed = mixed.astype(jnp.bfloat16)
                 re = jnp.dot(w, mixed[:antennas2], preferred_element_type=jnp.float32)
@@ -142,18 +201,19 @@
                 t = jnp.dot(high, gather_ref[m], preferred_element_type=jnp.float32)
                 t += jnp.dot(low, gather_ref[m], preferred_element_type=jnp.float32)
                 total = t if total is None else total + t
-            pbuf[k, :, q, c] = total.reshape(ng, 8, 128)
+            pbuf[k, :, c] = total.reshape(ng, 8, 128)
             return 0
 
-        lax.fori_loop(0, 2 * per, channel, 0)
-
-        pltpu.make_async_copy(pbuf.at[k, g], out_ref.at[:, g, k], pget).start()
+        lax.fori_loop(0, per, channel, 0)
+
+        target = out_ref.at[side, lax.rem(g + which * group, ng), part_of]
+        pltpu.make_async_copy(pbuf.at[k, g], target, pget).start()
 
         def send(i, _):
             d = lax.rem(g + i, ng)
             pltpu.make_async_remote_copy(
                 src_ref=pbuf.at[k, d],
-                dst_ref=out_ref.at[:, g, k],
+                dst_ref=target,
                 send_sem=psend,
                 recv_sem=pget,
                 device_id=(x, d),
@@ -164,14 +224,17 @@
         lax.fori_loop(1, ng, send, 0)
         return 0
 
-    lax.fori_loop(0, CHUNKS, chunk_step, 0)
+    lax.fori_loop(0, steps, step, 0)
 
     pltpu.make_async_copy(out_ref, out_ref, pget).wait()
-    for k in range(CHUNKS):
-        sent = sbuf.at[k, pl.ds(0, n - 1)]
+    for k in range(steps):
+        sent = sbuf.at[k, pl.ds(0, dests - 1)]
         pltpu.make_async_copy(sent, sent, vsend.at[k]).wait()
     sent = pbuf.at[:, pl.ds(0, ng - 1)]
     pltpu.make_async_copy(sent, sent, psend).wait()
+    sent = w_ref.at[1, pl.ds(0, PIECES * piece)]
+    pltpu.make_async_copy(sent, sent, wsend).wait()
+    pltpu.make_async_copy(sent, sent, relay_sem).wait()
 
 
 def spread_kernel(in_ref, out_ref):
@@ -216,13 +279,17 @@
         in_specs=[vmem, anywhere, vmem, vmem, vmem],
         out_specs=anywhere,
         scratch_shapes=[
-            pltpu.VMEM((CHUNKS, nx * ng, per, rows, half), jnp.bfloat16),
-            pltpu.VMEM((CHUNKS, nx * ng, per, rows, half), jnp.bfloat16),
+            pltpu.VMEM((2 * CHUNKS, nx * group, per, rows, half), jnp.bfloat16),
+            pltpu.VMEM((2 * CHUNKS, nx * group, per, rows, half), jnp.bfloat16),
             pltpu.VMEM(turned_weights.shape, jnp.bfloat16),
-            pltpu.VMEM((CHUNKS, ng, 2, per, 8, 128), jnp.float32),
-            pltpu.SemaphoreType.DMA,
-            pltpu.SemaphoreType.DMA((CHUNKS,)),
-            pltpu.SemaphoreType.DMA((CHUNKS,)),
+            pltpu.VMEM((2 * CHUNKS, ng, per, 8, 128), jnp.float32),
+            pltpu.SemaphoreType.DMA,
+            pltpu.SemaphoreType.DMA,
+            pltpu.SemaphoreType.DMA((PIECES,)),
+            pltpu.SemaphoreType.DMA,
+            pltpu.SemaphoreType.DMA,
+            pltpu.SemaphoreType.DMA((2 * CHUNKS,)),
+            pltpu.SemaphoreType.DMA((2 * CHUNKS,)),
             pltpu.SemaphoreType.DMA,
             pltpu.SemaphoreType.DMA,
         ],

time: 147 us -> 120 us (0.82)
  Pallas kernels: 146 us -> 120 us
    pallas_call x1, Pallas kernels: 143 us -> 117 us  [on_device(): pl.pallas_call(functools.partial(kernel, nx, ng), out_shape=jax.ShapeDtyp...]
where the time goes in v3:
time: 120 us
  Pallas kernels  120 us (100%)
    pallas_call x1, Pallas kernels, on_device(): pl.pallas_call(functools.partial(kernel, nx, ng), out_shape=jax.ShapeDtyp...  117 us
    pallas_call x1, Pallas kernels, on_device(): pl.pallas_call(spread_kernel, grid=(2,), out_shape=jax.ShapeDtypeStruct((...  2.9 us

profile of v3, /device:TPU:25, one launch (start us, length us, event | category | flops | bytes accessed | tf_op | source)
XLA Modules:
  0.0 119.8 jit_solution(2674309838933829367)
XLA Ops:
  0.0 116.9 %shard_map.55 = f32[2,16,4,4,8,128]{5,4,3,2,1,0:T(8,128)} custom-call(bf16[8,2,256,512]{3,2,1,0:T(8,128)(2,1)} %bitcast.5, bf16[2,16,2,64,512]{4,3,2,1,0:T(8,128)(2,1)} %bitcast.6, bf16[256,256]{1,0:T(8,128)(2,1)} %constant.6.clone.turn_ref, bf16[256,128]{1,0:T(8,128)(2,1)} %constant.7.clone.mix_ref, bf16[4,256,128]{2,1,0:T(8,128)(2,1)} %constant.8.clone.gather_ref), custom_call_target="tpu_custom_call" | custom-call | tf_op jit(solution)/shard_map/pallas_call | solution.py:276
  116.9 2.9 %shard_map.56 = f32[2,32,32,256]{3,2,1,0:T(8,128)} custom-call(f32[2,2048,128]{2,1,0:T(8,128)} %bitcast.4), custom_call_target="tpu_custom_call" | custom-call | tf_op jit(solution)/shard_map/pallas_call | solution.py:301
